TPU v7x, 512 devices: a whole 4x8x8 slice. The times are simulated.
512 devices in a mesh: gx: 8 (over y), gy: 64 (over x, z, core).
Axes of the slice: x: 4, y: 8, z: 8, core: 2. Of those that a mesh axis runs over, the one named last changes fastest.
Arguments:
- basis_mats: float32 [12, 275, 275], replicated, may hold values from -8 to 8.5, as said below
- coeffs: float32 [8192, 12], P(('gx', 'gy')), may hold values from 0.5 to 2
- element_loads: float32 [8192, 275], P(('gx', 'gy')), may hold values from -18 to 18
- elem_faces: int32 [8192, 6], P(('gx', 'gy')), may hold values from 0 to 71, as said below
- orient_codes: int32 [8192, 6], P(('gx', 'gy')), may hold values from 0 to 7
- shared_owned: int32 [512, 2, 4], P(('gx', 'gy')), may hold values from 0 to 63, as said below
- shared_remote: int32 [512, 2, 4], P(('gx', 'gy')), may hold values from 0 to 7, as said below
- lower_peers: int32 [512, 2], P(('gx', 'gy')), may hold values from 0 to 511, as said below
- upper_peers: int32 [512, 2], P(('gx', 'gy')), may hold values from 0 to 511, as said below
Outputs:
- trace: float32 [25, 32768], P(None, ('gx', 'gy'))
- residual: float32 [25, 32768], P(None, ('gx', 'gy'))
Inputs may be any that keep to these rules, and one draw needn't show every extreme that they name: `basis_mats`: each matrix is symmetric with every eigenvalue at least 0.5. `elem_faces`: an entry below 64 is a face slot that the element's device owns; an entry 64 + r is that device's remote slot r. Every owned slot of a device is named by one or two of its element faces, every remote slot by exactly one. `shared_owned`: row (d, i) lists 4 distinct owned slots of device d, in message order, that device lower_peers[d, i] uses; the two rows of a device are disjoint. `shared_remote`: row (d, i) lists remote slots of device d in message order: its k-th entry is the face that device upper_peers[d, i] lists k-th in its row i of shared_owned. The two rows of a device together hold each of its 8 remote slots once. upper_peers[lower_peers[d, i], i] = d for every device d and i; the two entries of a row differ. Peers are arbitrary device numbers. lower_peers[upper_peers[d, i], i] = d for every device d and i; the two entries of a row differ; each column is a permutation of the devices. Peers are arbitrary device numbers.
All inputs are finite; a program needn't handle non-finite values.
Results may differ from a plain program's by a relative error of at most 0.0003.
Values sent between devices are 32-bit elements; how exact they have to be, the bound alone decides.
No kernel may reach another device: no remote copies, remote signals or barrier semaphores. Data moves between devices by JAX's collectives and lax.ppermute only.
A program may use at most 128 MiB of HBM per device.

v0:
```python
import jax
import jax.numpy as jnp
import numpy as np
from jax import lax
from jax.experimental import pallas as pl
from jax.experimental.pallas import tpu as pltpu
from jax.sharding import PartitionSpec as P

SIDE = 5
FACE_DOFS = 25
CELL_DOFS = 125
TRACE_DOFS = 150
LOCAL_DOFS = 275
TERMS = 12
ITERS = 4
ELEM_DEV = 16
FACE_DEV = 64
SHARED = 4
REMOTE = 8
SLOTS = FACE_DEV + REMOTE
ROWS = 6 * ELEM_DEV
PIVOT = 16
CELL_PAD = 128
TRACE_PAD = 152
LOAD_LANE = TRACE_DOFS
WIDE = 256

INTERPRET = False
f32 = jnp.float32
bf16 = jnp.bfloat16


def thirds(x):
    high = x.astype(bf16)
    rest = x - high.astype(f32)
    middle = rest.astype(bf16)
    return high, middle, (rest - middle.astype(f32)).astype(bf16)


def left_parts(parts, axis=0):
    high, middle, low = parts
    return jnp.concatenate([high, high, middle, high, low, middle], axis=axis)


def right_parts(parts):
    high, middle, low = parts
    return jnp.concatenate([high, middle, high, low, high, middle], axis=0)


def product(a, b, contract=0):
    dims = (((contract,), (0,)), ((), ()))
    return lax.dot_general(a, b, dims, preferred_element_type=f32)


def pick_left(mask, x):
    return sum(jnp.dot(mask, part, preferred_element_type=f32) for part in thirds(x))


def pick_right(x, mask, contract=0):
    dims = (((1,), (contract,)), ((), ()))
    return sum(lax.dot_general(part, mask, dims, preferred_element_type=f32) for part in thirds(x))


def orient_table():
    n = SIDE
    table = np.zeros((8, n * n), np.int32)
    for code in range(8):
        for a in range(n):
            for b in range(n):
                a2, b2 = (b, a) if code & 1 else (a, b)
                if code & 2:
                    a2 = n - 1 - a2
                if code & 4:
                    b2 = n - 1 - b2
                table[code, a * n + b] = a2 * n + b2
    return table


def place_matrix():
    table = orient_table()
    place = np.zeros((WIDE, WIDE), np.float32)
    for code in range(8):
        for q in range(FACE_DOFS):
            for j in range(6):
                place[code * 32 + table[code, q], j * FACE_DOFS + q] = 1.0
    return place


def iota(shape, axis):
    return lax.broadcasted_iota(jnp.int32, shape, axis)


def retile(x):
    x = x + pltpu.roll(x, 64, 1)
    return x + pltpu.roll(x, 32, 1)


def spread(field, pick, valid, place):
    rows = pick_left(pick, field)
    rows = jnp.concatenate([rows, rows], axis=1) * valid
    placed = pick_right(rows, place)
    lane = iota((ELEM_DEV, WIDE), 1)
    total = jnp.zeros((ELEM_DEV, WIDE), f32)
    for j in range(6):
        mine = (lane >= j * FACE_DOFS) & (lane < (j + 1) * FACE_DOFS)
        total = jnp.where(mine, placed[j * ELEM_DEV : (j + 1) * ELEM_DEV], total)
    return total


def collect(values, pick_t, valid, place):
    lane = iota((ELEM_DEV, WIDE), 1)
    parts = []
    for j in range(6):
        mine = (lane >= j * FACE_DOFS) & (lane < (j + 1) * FACE_DOFS)
        parts.append(jnp.where(mine, values, 0.0))
    turned = pick_right(jnp.concatenate(parts, axis=0), place, 1) * valid
    summed = pick_left(pick_t, turned)
    return retile(summed[:, :128] + summed[:, 128:])


class Links:
    def __init__(self, owned_ref, remote_ref, lower_ref, upper_ref):
        self.owned, self.remote, self.lower, self.upper = owned_ref, remote_ref, lower_ref, upper_ref

    def peer(self, m):
        return (self.lower if m < 2 else self.upper)[0, m % 2]

    def slot(self, m, k):
        if m < 2:
            return self.owned[0, m, k]
        return FACE_DEV + self.remote[0, m - 2, k]

    def clash(self):
        hits = [jnp.where(self.peer(i) == self.peer(2 + j), 1, 0) for i in range(2) for j in range(2)]
        return jnp.where(hits[0] + hits[1] + hits[2] + hits[3] > 0, 1.0, 0.0)


def message(ref, links, m):
    block = iota((1, 128), 1) // 32
    row = ref[pl.ds(links.slot(m, 0), 1), :]
    for k in range(1, SHARED):
        row = jnp.where(block == k, ref[pl.ds(links.slot(m, k), 1), :], row)
    return row


def settle(ref, incoming, links):
    block = iota((1, 128), 1) // 32
    inside = iota((1, 128), 1) % 32 < FACE_DOFS
    rows = []
    for m in range(4):
        row = jnp.where(inside, incoming[m], 0.0)
        for k in range(SHARED):
            rows.append(jnp.where(block == k, row, 0.0))
    rows = retile(jnp.concatenate(rows, axis=0))
    for m in range(4):
        for k in range(SHARED):
            at = pl.ds(links.slot(m, k), 1)
            ref[at, :] = ref[at, :] + rows[m * SHARED + k : m * SHARED + k + 1]


def write_bucket(out_ref, fill, links, rows, wide):
    count = len(rows[0])
    out_ref[...] = jnp.broadcast_to(fill, out_ref.shape)
    keep = iota((1, 128), 1) % 32 < FACE_DOFS
    for m in range(4):
        start = links.peer(m) * (2 * count if wide else count) + (count * (m // 2) if wide else 0)
        for n in range(count):
            out_ref[pl.ds(start + n, 1), :] = jnp.where(keep, rows[m][n], fill)


def read_bucket(in_ref, links, count, n, wide):
    got = []
    for m in range(4):
        start = links.peer(m) * (2 * count if wide else count) + (count * (1 - m // 2) if wide else 0)
        got.append(in_ref[pl.ds(start + n, 1), :])
    return got


def invert_blocks(x):
    n = PIVOT
    halves = n // 8
    sub = iota((8, 128), 0)
    for k in range(n):
        kh, ks = k // 8, k % 8
        hit = sub == ks
        factors = [jnp.broadcast_to(x[i][kh][ks : ks + 1], (8, 128)) for i in range(n)]
        inv = 1.0 / factors[k]
        lead = [x[k][h] * inv for h in range(halves)]
        lead[kh] = jnp.where(hit, inv, lead[kh])
        for i in range(n):
            if i == k:
                continue
            for h in range(halves):
                old = jnp.where(hit, 0.0, x[i][h]) if h == kh else x[i][h]
                x[i][h] = old - factors[i] * lead[h]
        x[k] = lead
    return x


def condense_kernel(
    coeffs_ref,
    owned_ref,
    remote_ref,
    lower_ref,
    upper_ref,
    basis_ref,
    loads_ref,
    faces_ref,
    codes_ref,
    place_ref,
    schur_ref,
    fields_ref,
    pick_ref,
    pick_t_ref,
    valid_ref,
    bucket_ref,
    shifted_ref,
    panel_ref,
    scaled_ref,
    inverse_ref,
    diag_ref,
    load_ref,
    terms_ref,
    copies,
):
    links = Links(owned_ref, remote_ref, lower_ref, upper_ref)
    width = CELL_PAD + WIDE

    def copy_in(k):
        return pltpu.make_async_copy(basis_ref.at[k], terms_ref.at[k], copies.at[k])

    for k in range(TERMS):
        copy_in(k).start()

    def shift(k, carry):
        copy_in(k).wait()
        shifted_ref[k, 0:128, 0:125] = terms_ref[k, 0:128, 0:125]
        shifted_ref[k, 0:128, 125:128] = jnp.zeros((128, 3), f32)
        shifted_ref[k, 0:128, 128:278] = terms_ref[k, 0:128, 125:275]
        shifted_ref[k, 0:128, 278:384] = jnp.zeros((128, 106), f32)
        shifted_ref[k, 128:278, 128:278] = terms_ref[k, 125:275, 125:275]
        shifted_ref[k, 128:280, 278:384] = jnp.zeros((152, 106), f32)
        return carry

    lax.fori_loop(0, TERMS, shift, 0)

    def cell_rows(g, carry):
        at = pl.ds(pl.multiple_of(g * 8, 8), 8)
        terms = [shifted_ref[k, at, :] for k in range(TERMS)]
        for e in range(ELEM_DEV):
            total = coeffs_ref[e, 0] * terms[0]
            for k in range(1, TERMS):
                total = total + coeffs_ref[e, k] * terms[k]
            panel_ref[e, at, :] = total
        return carry

    lax.fori_loop(0, CELL_PAD // 8, cell_rows, 0)

    def trace_rows(g, carry):
        at = pl.ds(pl.multiple_of(g * 8, 8), 8)
        source = pl.ds(pl.multiple_of(CELL_PAD + g * 8, 8), 8)
        terms = [shifted_ref[k, source, CELL_PAD:] for k in range(TERMS)]
        for e in range(ELEM_DEV):
            total = coeffs_ref[e, 0] * terms[0]
            for k in range(1, TERMS):
                total = total + coeffs_ref[e, k] * terms[k]
            schur_ref[e, at, :] = total
        return carry

    lax.fori_loop(0, TRACE_PAD // 8, trace_rows, 0)

    unit = (iota((3, width), 1) == iota((3, width), 0) + CELL_DOFS).astype(f32)
    load_lane = iota((CELL_PAD, 128), 1) == (CELL_PAD + LOAD_LANE) % 128
    pad = jnp.zeros((128 - ELEM_DEV, 128), f32)
    load_cols = jnp.concatenate([loads_ref[:, 0:128], pad], axis=0).T
    for e in range(ELEM_DEV):
        column = jnp.broadcast_to(load_cols[:, e : e + 1], (CELL_PAD, 128))
        panel_ref[e, :, 256:384] = jnp.where(load_lane, column, panel_ref[e, :, 256:384])
        panel_ref[e, CELL_DOFS:CELL_PAD, :] = unit
        schur_ref[e, LOAD_LANE:TRACE_PAD, :] = jnp.zeros((TRACE_PAD - LOAD_LANE, WIDE), f32)
        schur_ref[e, LOAD_LANE : LOAD_LANE + 1, 0:TRACE_DOFS] = loads_ref[e : e + 1, CELL_DOFS:LOCAL_DOFS]

    group = iota((ELEM_DEV, 128), 1) // PIVOT
    scaled_ref[...] = jnp.zeros(scaled_ref.shape, bf16)

    def folded(x):
        return x[0:PIVOT] + (x[PIVOT : 2 * PIVOT] + x[2 * PIVOT : 3 * PIVOT])

    for step in range(CELL_PAD // PIVOT):
        base = step * PIVOT
        own = slice(base, base + PIVOT)
        if step > 0:
            for e in range(ELEM_DEV):
                depth = 32 if base <= 32 else 64 if base <= 64 else 128
                left = panel_ref[e, 0:base, 0:128].T[own]
                if base < 128:
                    left = jnp.concatenate([left, jnp.zeros((PIVOT, 128 - base), f32)], axis=1)
                if depth == 128:
                    left = jnp.concatenate([left, left, left], axis=1)
                elif depth == 64:
                    left = jnp.concatenate([left + pltpu.roll(left, 64, 1), left], axis=1)
                else:
                    left = left + pltpu.roll(left, 32, 1) + pltpu.roll(left, 64, 1)
                lane = iota(left.shape, 1)
                stacked = jnp.concatenate(
                    [
                        jnp.where(lane < (3 - n) * depth, part.astype(f32), 0.0).astype(bf16)
                        for n, part in enumerate(thirds(left))
                    ],
                    axis=0,
                )[:, 0 : 3 * depth]
                right = jnp.concatenate([scaled_ref[n, e, 0:depth, :] for n in range(3)], axis=0)
                panel_ref[e, own, :] = panel_ref[e, own, :] - folded(product(stacked, right, 1))
        x = []
        for half in range(PIVOT // 8):
            packed = jnp.zeros((ELEM_DEV, 128), f32)
            for s in range(8):
                slab = panel_ref[:, base + half * 8 + s, 0:128]
                turn = (s * PIVOT - base) % 128
                if turn:
                    slab = pltpu.roll(slab, turn, 1)
                packed = jnp.where(group == s, slab, packed)
            tall = jnp.concatenate([packed, jnp.zeros((128 - ELEM_DEV, 128), f32)], axis=0).T
            for s in range(8):
                x.append([tall[s * PIVOT + 8 * h : s * PIVOT + 8 * h + 8] for h in range(PIVOT // 8)])
        x = invert_blocks(x)
        for half in range(PIVOT // 8):
            tall = jnp.concatenate([v for s in range(8) for v in x[half * 8 + s]], axis=0)
            packed = tall.T[:ELEM_DEV]
            for s in range(8):
                first, second, third = (
                    pltpu.roll(packed, (t - s) * PIVOT % 128, 1) if (t - s) % 8 else packed for t in range(3)
                )
                inverse_ref[:, half * 8 + s, :] = jnp.where(group == 0, first, jnp.where(group == 1, second, third))
        for e in range(ELEM_DEV):
            top = panel_ref[e, own, :]
            parts = thirds(inverse_ref[e])
            stacked = jnp.concatenate(
                [
                    jnp.where(group < 3 - n, part.astype(f32), 0.0).astype(bf16)
                    for n, part in enumerate(parts)
                ],
                axis=0,
            )
            right = jnp.concatenate(thirds(top), axis=0)
            scaled = thirds(folded(product(stacked[:, 0 : 3 * PIVOT], right, 1)))
            for n in range(3):
                scaled_ref[n, e, own, :] = scaled[n]

    diagonal = iota((TRACE_PAD, WIDE), 0) == iota((TRACE_PAD, WIDE), 1)

    def finish(e, carry):
        left = panel_ref[e, :, CELL_PAD : CELL_PAD + WIDE].T[:TRACE_PAD]
        right = right_parts([scaled_ref[n, e, :, CELL_PAD : CELL_PAD + WIDE] for n in range(3)])
        block = schur_ref[e] - product(left_parts(thirds(left), 1), right, 1)
        schur_ref[e] = block
        at = pl.ds(e, 1)
        diag_ref[at] = jnp.sum(jnp.where(diagonal, block, 0.0), axis=0, keepdims=True)[None]
        load_ref[at] = block[LOAD_LANE : LOAD_LANE + 1][None]
        return carry

    lax.fori_loop(0, ELEM_DEV, finish, 0, unroll=4)

    faces_row = faces_ref[...].astype(f32)
    square = jnp.zeros((122, 128), f32)
    fill = jnp.zeros((6, 128 - ELEM_DEV), f32)
    faces_t = jnp.concatenate([jnp.concatenate([faces_row, fill], axis=1), square], axis=0).T
    codes_t = jnp.concatenate([jnp.concatenate([codes_ref[...].astype(f32), fill], axis=1), square], axis=0).T
    slots_col = jnp.concatenate([faces_t[:ELEM_DEV, j : j + 1] for j in range(6)], axis=0)
    codes_col = jnp.concatenate([codes_t[:ELEM_DEV, j : j + 1] for j in range(6)], axis=0)
    slots_row = jnp.concatenate([faces_row[j : j + 1] for j in range(6)], axis=1)
    pick_ref[...] = jnp.where(iota((ROWS, SLOTS), 1).astype(f32) == slots_col, 1.0, 0.0).astype(bf16)
    pick_t_ref[...] = jnp.where(iota((SLOTS, ROWS), 0).astype(f32) == slots_row, 1.0, 0.0).astype(bf16)
    lanes = iota((ROWS, WIDE), 1)
    valid = ((lanes // 32).astype(f32) == codes_col) & (lanes % 32 < FACE_DOFS)
    valid_ref[...] = jnp.where(valid, 1.0, 0.0)

    inside = iota((ELEM_DEV, WIDE), 1) < TRACE_DOFS
    for n, ref in enumerate((load_ref, diag_ref)):
        values = jnp.where(inside, ref[...].reshape(ELEM_DEV, WIDE), 0.0)
        fields_ref[n] = collect(values, pick_t_ref[...], valid_ref[...], place_ref[...])
    send_fields(fields_ref, links, bucket_ref, False)


def send_fields(fields_ref, links, bucket_ref, wide):
    rows = [[message(fields_ref.at[n], links, m) for n in range(2)] for m in range(4)]
    fill = jnp.where(iota((1, 128), 1) == 25, links.clash(), 0.0)
    write_bucket(bucket_ref, fill, links, rows, wide)


def resend_kernel(owned_ref, remote_ref, lower_ref, upper_ref, fields_ref, bucket_ref):
    send_fields(fields_ref, Links(owned_ref, remote_ref, lower_ref, upper_ref), bucket_ref, True)


def sum_rows(x):
    total = x[0:8]
    for at in range(8, x.shape[0], 8):
        total = total + x[at : at + 8]
    return jnp.sum(total, axis=0, keepdims=True)


def total_of(x):
    return jnp.sum(jnp.sum(x, axis=0, keepdims=True), axis=1, keepdims=True)


def apply_and_send(r, z, q, links, fixed, partial_ref, bucket_ref, image_ref, wide):
    schur_ref, pick_ref, pick_t_ref, valid_ref, place_ref = fixed
    x = spread(z, pick_ref[...], valid_ref[...], place_ref[...])
    pad = jnp.zeros((128 - ELEM_DEV, 128), f32)
    head = jnp.concatenate([x[:, 0:128], pad], axis=0).T
    tail = jnp.concatenate([x[:, 128:256], pad], axis=0).T[: TRACE_PAD - 128]
    columns = jnp.concatenate([head, tail], axis=0)
    for e in range(ELEM_DEV):
        image_ref[e : e + 1, :] = jnp.sum(schur_ref[e] * columns[:, e : e + 1], axis=0, keepdims=True)
    images = image_ref[...]
    quad = total_of(x * images)
    own = iota((FACE_DEV, 128), 1) < FACE_DOFS
    rz = total_of(jnp.where(own, r[:FACE_DEV] * z[:FACE_DEV], 0.0))
    zq = total_of(jnp.where(own, z[:FACE_DEV] * q[:FACE_DEV], 0.0))
    partial_ref[...] = collect(images, pick_t_ref[...], valid_ref[...], place_ref[...])
    rows = [[message(partial_ref, links, m)] for m in range(4)]
    lane = iota((1, 128), 1)
    sums = jnp.where(lane == 25, quad, jnp.where(lane == 26, rz, jnp.where(lane == 27, zq, 0.0)))
    write_bucket(bucket_ref, sums, links, rows, wide)


def start_kernel(wide, owned_ref, remote_ref, lower_ref, upper_ref, fields_in_ref, arrived_ref, *refs):
    links = Links(owned_ref, remote_ref, lower_ref, upper_ref)
    fixed, (state_ref, partial_ref, bucket_ref, clash_ref, fields_ref, image_ref) = refs[:5], refs[5:]
    clash_ref[0] = jnp.sum(sum_rows(arrived_ref[...])[:, 25:26])
    fields_ref[...] = fields_in_ref[...]
    for n in range(2):
        settle(fields_ref.at[n], read_bucket(arrived_ref, links, 2, n, wide), links)
    inside = iota((SLOTS, 128), 1) % 32 < FACE_DOFS
    r = jnp.where(inside, fields_ref[0], 0.0)
    diag = jnp.where(inside, fields_ref[1], 1.0)
    zero = jnp.zeros((SLOTS, 128), f32)
    z = r / diag
    state_ref[0] = zero
    state_ref[1] = zero
    state_ref[2] = r
    state_ref[3] = zero
    state_ref[4] = diag
    state_ref[5] = jnp.where(iota((SLOTS, 128), 0) == 0, jnp.inf, 0.0)
    apply_and_send(r, z, zero, links, fixed, partial_ref, bucket_ref, image_ref, wide)


def advance(wide, links, partial_in_ref, arrived_ref, state_ref, work_ref):
    work_ref[...] = partial_in_ref[...]
    settle(work_ref, read_bucket(arrived_ref, links, 1, 0, wide), links)
    sums = sum_rows(arrived_ref[...])
    if wide:
        sums = sums * 0.5
    quad, rz, zq = sums[:, 25:26], sums[:, 26:27], sums[:, 27:28]
    old_rz, old_energy = state_ref[5, 0:1, 0:1], state_ref[5, 1:2, 0:1]
    beta = rz / old_rz
    direction = state_ref[2] / state_ref[4] + beta * state_ref[1]
    image = work_ref[...] + beta * state_ref[3]
    energy = quad + 2.0 * beta * zq + beta * beta * old_energy
    alpha = rz / energy
    trace = state_ref[0] + alpha * direction
    residual = state_ref[2] - alpha * image
    return trace, direction, residual, image, rz, energy


def step_kernel(wide, owned_ref, remote_ref, lower_ref, upper_ref, partial_in_ref, arrived_ref, state_in_ref, *refs):
    links = Links(owned_ref, remote_ref, lower_ref, upper_ref)
    fixed, (state_ref, partial_ref, bucket_ref, work_ref, image_ref) = refs[:5], refs[5:]
    trace, direction, residual, image, rz, energy = advance(
        wide, links, partial_in_ref, arrived_ref, state_in_ref, work_ref
    )
    diag = state_in_ref[4]
    state_ref[0] = trace
    state_ref[1] = direction
    state_ref[2] = residual
    state_ref[3] = image
    state_ref[4] = diag
    state_ref[5] = jnp.where(iota((SLOTS, 128), 0) == 0, rz, energy)
    apply_and_send(
        residual, residual / diag, image, links, fixed, partial_ref, bucket_ref, image_ref, wide
    )


def finish_kernel(
    wide, owned_ref, remote_ref, lower_ref, upper_ref, partial_in_ref, arrived_ref, state_in_ref,
    trace_ref, residual_ref, work_ref,
):
    links = Links(owned_ref, remote_ref, lower_ref, upper_ref)
    trace, _, residual, _, _, _ = advance(wide, links, partial_in_ref, arrived_ref, state_in_ref, work_ref)
    pad = jnp.zeros((128 - FACE_DEV, 128), f32)
    trace_ref[...] = jnp.concatenate([trace[:FACE_DEV], pad], axis=0).T[:FACE_DOFS, :FACE_DEV]
    residual_ref[...] = jnp.concatenate([residual[:FACE_DEV], pad], axis=0).T[:FACE_DOFS, :FACE_DEV]


VMEM = pl.BlockSpec(memory_space=pltpu.VMEM)
SMEM = pl.BlockSpec(memory_space=pltpu.SMEM)
HBM = pl.BlockSpec(memory_space=pltpu.HBM)


def shape(*dims, dtype=f32):
    return jax.ShapeDtypeStruct(dims, dtype)


def call(body, name, scalars, arrays, outs, scratch, specs=None, out_specs=None, grant=12):
    return pl.pallas_call(
        body,
        name=name,
        in_specs=[SMEM] * len(scalars) + (specs or [VMEM] * len(arrays)),
        out_specs=out_specs or [VMEM] * len(outs),
        out_shape=outs,
        scratch_shapes=[pltpu.VMEM(item, f32) if isinstance(item, tuple) else item for item in scratch],
        compiler_params=pltpu.CompilerParams(vmem_limit_bytes=grant << 20),
        interpret=INTERPRET,
    )(*scalars, *arrays)


def on_device(
    basis_mats,
    coeffs,
    element_loads,
    elem_faces,
    orient_codes,
    shared_owned,
    shared_remote,
    lower_peers,
    upper_peers,
):
    axes = ("gx", "gy")
    devices = lax.axis_size("gx") * lax.axis_size("gy")
    links = (shared_owned, shared_remote, lower_peers, upper_peers)
    place = jnp.asarray(place_matrix(), bf16)
    width = CELL_PAD + WIDE

    def exchange_twice(bucket):
        grid = (lax.axis_size("gx"), lax.axis_size("gy"), bucket.shape[0] // devices, 128)
        sent = lax.all_to_all(bucket.reshape(grid), "gx", split_axis=0, concat_axis=0, tiled=True)
        return lax.all_to_all(sent, "gy", split_axis=1, concat_axis=1, tiled=True).reshape(bucket.shape)

    def exchange(bucket):
        parts = bucket.shape[0] // devices
        sent = bucket.reshape(devices, parts, 128) if parts > 1 else bucket
        got = lax.all_to_all(sent, axes, split_axis=0, concat_axis=0, tiled=True)
        return got.reshape(bucket.shape)

    schur, fields, pick, pick_t, valid, bucket = call(
        condense_kernel,
        "condense",
        (coeffs,) + links,
        (pltpu.with_memory_space_constraint(basis_mats, pltpu.HBM), element_loads, elem_faces.T, orient_codes.T, place),
        (
            shape(ELEM_DEV, TRACE_PAD, WIDE),
            shape(2, SLOTS, 128),
            shape(ROWS, SLOTS, dtype=bf16),
            shape(SLOTS, ROWS, dtype=bf16),
            shape(ROWS, WIDE),
            shape(2 * devices, 128),
        ),
        (
            (TERMS, CELL_PAD + TRACE_PAD, width),
            (ELEM_DEV, CELL_PAD, width),
            pltpu.VMEM((3, ELEM_DEV, CELL_PAD, width), bf16),
            (ELEM_DEV, PIVOT, 128),
            (ELEM_DEV, 1, WIDE),
            (ELEM_DEV, 1, WIDE),
            (TERMS, LOCAL_DOFS, LOCAL_DOFS),
            pltpu.SemaphoreType.DMA((TERMS,)),
        ),
        specs=[HBM] + [VMEM] * 4,
        grant=44,
    )
    fixed = (schur, pick, pick_t, valid, place)

    def start(arrived, wide):
        return call(
            lambda *refs: start_kernel(wide, *refs),
            "start_wide" if wide else "start",
            links,
            (fields, arrived) + fixed,
            (shape(6, SLOTS, 128), shape(SLOTS, 128), shape((1 + wide) * devices, 128), shape(1)),
            ((2, SLOTS, 128), (ELEM_DEV, WIDE)),
            out_specs=[VMEM] * 3 + [SMEM],
        )

    def step(state, partial_value, arrived, wide):
        return call(
            lambda *refs: step_kernel(wide, *refs),
            "step_wide" if wide else "step",
            links,
            (partial_value, arrived, state) + fixed,
            (shape(6, SLOTS, 128), shape(SLOTS, 128), shape((1 + wide) * devices, 128)),
            ((SLOTS, 128), (ELEM_DEV, WIDE)),
        )

    def finish(state, partial_value, arrived, wide):
        return tuple(
            call(
                lambda *refs: finish_kernel(wide, *refs),
                "finish_wide" if wide else "finish",
                links,
                (partial_value, arrived, state),
                (shape(FACE_DOFS, FACE_DEV), shape(FACE_DOFS, FACE_DEV)),
                ((SLOTS, 128),),
            )
        )

    def narrow_run(state, partial_value, bucket):
        def body(_, carry):
            state, partial_value, bucket = carry
            return tuple(step(state, partial_value, exchange(bucket), False))

        carry = lax.fori_loop(0, ITERS - 1, body, (state, partial_value, bucket))
        state, partial_value, bucket = carry
        return finish(state, partial_value, exchange(bucket), False)

    def wide_run(state, partial_value, bucket):
        (again,) = call(resend_kernel, "resend", links, (fields,), (shape(4 * devices, 128),), ())
        state, partial_value, bucket, _ = start(exchange_twice(again), True)

        def body(_, carry):
            state, partial_value, bucket = carry
            return tuple(step(state, partial_value, exchange_twice(bucket), True))

        carry = lax.fori_loop(0, ITERS, body, (state, partial_value, bucket))
        return carry[0][0, :FACE_DEV, :FACE_DOFS].T, carry[0][2, :FACE_DEV, :FACE_DOFS].T

    state, partial_value, bucket, clash = start(exchange(bucket), False)
    return lax.cond(clash[0] > 0.0, wide_run, narrow_run, state, partial_value, bucket)


def solution(mesh):
    placed = (
        P(),
        P(("gx", "gy"), None),
        P(("gx", "gy"), None),
        P(("gx", "gy"), None),
        P(("gx", "gy"), None),
        P(("gx", "gy"), None, None),
        P(("gx", "gy"), None, None),
        P(("gx", "gy"), None),
        P(("gx", "gy"), None),
    )
    return jax.shard_map(
        on_device,
        mesh=mesh,
        in_specs=placed,
        out_specs=(P(None, ("gx", "gy")), P(None, ("gx", "gy"))),
        check_vma=False,
    )
```

profile of v0, /device:TPU:1, one launch (start us, length us, event | category | flops | bytes accessed | tf_op | source)
XLA Modules:
  0.0 197.5 jit_solution(16620315156981445079)
XLA Ops:
  0.6 0.0 copy-start.4
  0.6 0.0 copy-start.5
  0.7 0.0 copy-start.6
  0.7 0.0 copy-start.7
  0.7 0.0 copy-start
  0.7 0.8 copy-done
  1.4 0.0 copy-start.1
  1.4 0.7 copy-done.1
  2.1 0.0 copy-start.2
  2.1 0.7 copy-done.2
  2.8 0.0 copy-start.3
  2.8 0.7 copy-done.3
  3.5 26.7 %condense.1 = (f32[16,152,256]{2,1,0:T(8,128)S(1)}, f32[2,72,128]{2,1,0:T(8,128)S(1)}, bf16[96,72]{1,0:T(8,128)(2,1)S(1)}, bf16[72,96]{1,0:T(8,128)(2,1)S(1)}, f32[96,256]{1,0:T(8,128)}, /*index=5*/f32[1024,128]{1,0:T(8,128)}) custom-call(f32[16,12]{1,0:T(8,128)S(1)} %copy-done.1, s32[1,2,4]{2,1,0:T(2,128)} %refs_0_.1, s32[1,2,4]{2,1,0:T(2,128)} %refs_1_.1, ...), custom_call_target="tpu_custom_call" | custom-call | tf_op jit(solution)/shard_map/condense/pallas_call | solution.py:505
  30.2 22.2 %all-to-all-start.6 = ((f32[512,2,128]{2,1,0:T(2,128)}), f32[512,2,128]{2,1,0:T(2,128)S(1)}, u32[]{:S(2)}, u32[]{:S(2)}) async-start(f32[512,2,128]{2,1,0:T(2,128)} %bitcast.16), calls=%async_computation.6 | async-start | bytes 1048576 | tf_op jit(solution)/shard_map/all_to_all | solution.py:542
  52.4 22.7 %all-to-all-done.6 = f32[512,2,128]{2,1,0:T(2,128)S(1)} async-done(((f32[512,2,128]{2,1,0:T(2,128)}), f32[512,2,128]{2,1,0:T(2,128)S(1)}, u32[]{:S(2)}, u32[]{:S(2)}) %all-to-all-start.6) | async-done | bytes 524320 | tf_op jit(solution)/shard_map/all_to_all | solution.py:542
  75.1 0.0 copy-done.4
  75.1 0.0 copy-done.5
  75.1 0.0 copy-done.6
  75.1 0.0 copy-done.7
  75.1 3.7 %start.1 = (f32[6,72,128]{2,1,0:T(8,128)S(1)}, f32[72,128]{1,0:T(8,128)S(1)}, f32[512,128]{1,0:T(8,128)}, f32[1]{0:T(128)}) custom-call(s32[1,2,4]{2,1,0:T(2,128)S(1)} %copy-done.4, s32[1,2,4]{2,1,0:T(2,128)S(1)} %copy-done.5, s32[1,2]{1,0:T(1,128)S(1)} %copy-done.6, s32[1,2]{1,0:T(1,128)S(1)} %copy-done.7, f32[2,72,128]{2,1,0:T(8,128)S(1)} %get-tuple-element.223.refs_4_, ...), custom_call_target="tpu_custom_call" | custom-call | tf_op jit(solution)/shard_map/start/pallas_call | solution.py:505
  79.5 116.8 %conditional.1 = ((f32[25,64]{1,0:T(8,128)S(1)}, f32[25,64]{1,0:T(8,128)S(1)})) conditional(s32[]{:T(128)} %bitcast.18, (s32[1,2,4]{2,1,0:T(2,128)S(1)}, s32[1,2,4]{2,1,0:T(2,128)S(1)}, s32[1,2]{1,0:T(1,128)S(1)}, s32[1,2]{1,0:T(1,128)S(1)}, f32[16,152,256]{2,1,0:T(8,128)S(1)}, /*index=5*/bf16[96,72]{1,0:T(8,128)(2,1)S(1)}, ...), branch_computations={%region_0.0_spmd, %region_3.0_spmd} | conditional | flops 2 | bytes 14723413 | solution.py:627
  79.5 88.7 %while.26 = (s32[]{:T(128)}, f32[6,72,128]{2,1,0:T(8,128)S(1)}, f32[72,128]{1,0:T(8,128)S(1)}, f32[512,128]{1,0:T(8,128)}, s32[1,2,4]{2,1,0:T(2,128)S(1)}, /*ind...) while((s32[]{:T(128)}, f32[6,72,128]{2,1,0:T(8,128)S(1)}, ...), condition=%wide.region_2.0_spmd, body=%wide.region_1.0_spmd.sunk | while | flops 2 | bytes 1302693 | solution.py:611
  79.5 8.4 %all-to-all-start.4 = ((f32[512,1,128]{2,1,0:T(1,128)}), f32[512,1,128]{2,1,0:T(1,128)S(1)}, u32[]{:S(2)}, u32[]{:S(2)}) async-start(f32[512,1,128]{2,1,0:T(1,128)} %bitcast.27), calls=%async_computation.4 | async-start | bytes 524288 | tf_op jit(solution)/shard_map/cond/branch_0_fun/while/body/eval_jaxpr/all_to_all | solution.py:542
  87.9 17.0 %all-to-all-done.4 = f32[512,1,128]{2,1,0:T(1,128)S(1)} async-done(((f32[512,1,128]{2,1,0:T(1,128)}), f32[512,1,128]{2,1,0:T(1,128)S(1)}, u32[]{:S(2)}, u32[]{:S(2)}) %all-to-all-start.4) | async-done | bytes 262176 | tf_op jit(solution)/shard_map/cond/branch_0_fun/while/body/eval_jaxpr/all_to_all | solution.py:542
  104.9 3.8 %step.1 = (f32[6,72,128]{2,1,0:T(8,128)S(1)}, f32[72,128]{1,0:T(8,128)S(1)}, f32[512,128]{1,0:T(8,128)}) custom-call(s32[1,2,4]{2,1,0:T(2,128)S(1)} %get-tuple-element.553.refs_0_, s32[1,2,4]{2,1,0:T(2,128)S(1)} %get-tuple-element.554.refs_1_, s32[1,2]{1,0:T(1,128)S(1)} %get-tuple-element.555.refs_2_, s32[1,2]{1,0:T(1,128)S(1)} %get-tuple-element.556.refs_3_, ...), custom_call_target="tpu_custom_call" | custom-call | tf_op jit(solution)/shard_map/cond/branch_0_fun/while/body/eval_jaxpr/step/pallas_call | solution.py:505
  108.7 8.4 %all-to-all-start.4 = ((f32[512,1,128]{2,1,0:T(1,128)}), f32[512,1,128]{2,1,0:T(1,128)S(1)}, u32[]{:S(2)}, u32[]{:S(2)}) async-start(f32[512,1,128]{2,1,0:T(1,128)} %bitcast.27), calls=%async_computation.4 | async-start | bytes 524288 | tf_op jit(solution)/shard_map/cond/branch_0_fun/while/body/eval_jaxpr/all_to_all | solution.py:542
  117.1 17.5 %all-to-all-done.4 = f32[512,1,128]{2,1,0:T(1,128)S(1)} async-done(((f32[512,1,128]{2,1,0:T(1,128)}), f32[512,1,128]{2,1,0:T(1,128)S(1)}, u32[]{:S(2)}, u32[]{:S(2)}) %all-to-all-start.4) | async-done | bytes 262176 | tf_op jit(solution)/shard_map/cond/branch_0_fun/while/body/eval_jaxpr/all_to_all | solution.py:542
  134.6 3.8 %step.1 = (f32[6,72,128]{2,1,0:T(8,128)S(1)}, f32[72,128]{1,0:T(8,128)S(1)}, f32[512,128]{1,0:T(8,128)}) custom-call(s32[1,2,4]{2,1,0:T(2,128)S(1)} %get-tuple-element.553.refs_0_, s32[1,2,4]{2,1,0:T(2,128)S(1)} %get-tuple-element.554.refs_1_, s32[1,2]{1,0:T(1,128)S(1)} %get-tuple-element.555.refs_2_, s32[1,2]{1,0:T(1,128)S(1)} %get-tuple-element.556.refs_3_, ...), custom_call_target="tpu_custom_call" | custom-call | tf_op jit(solution)/shard_map/cond/branch_0_fun/while/body/eval_jaxpr/step/pallas_call | solution.py:505
  138.4 8.4 %all-to-all-start.4 = ((f32[512,1,128]{2,1,0:T(1,128)}), f32[512,1,128]{2,1,0:T(1,128)S(1)}, u32[]{:S(2)}, u32[]{:S(2)}) async-start(f32[512,1,128]{2,1,0:T(1,128)} %bitcast.27), calls=%async_computation.4 | async-start | bytes 524288 | tf_op jit(solution)/shard_map/cond/branch_0_fun/while/body/eval_jaxpr/all_to_all | solution.py:542
  146.9 17.5 %all-to-all-done.4 = f32[512,1,128]{2,1,0:T(1,128)S(1)} async-done(((f32[512,1,128]{2,1,0:T(1,128)}), f32[512,1,128]{2,1,0:T(1,128)S(1)}, u32[]{:S(2)}, u32[]{:S(2)}) %all-to-all-start.4) | async-done | bytes 262176 | tf_op jit(solution)/shard_map/cond/branch_0_fun/while/body/eval_jaxpr/all_to_all | solution.py:542
  164.3 3.8 %step.1 = (f32[6,72,128]{2,1,0:T(8,128)S(1)}, f32[72,128]{1,0:T(8,128)S(1)}, f32[512,128]{1,0:T(8,128)}) custom-call(s32[1,2,4]{2,1,0:T(2,128)S(1)} %get-tuple-element.553.refs_0_, s32[1,2,4]{2,1,0:T(2,128)S(1)} %get-tuple-element.554.refs_1_, s32[1,2]{1,0:T(1,128)S(1)} %get-tuple-element.555.refs_2_, s32[1,2]{1,0:T(1,128)S(1)} %get-tuple-element.556.refs_3_, ...), custom_call_target="tpu_custom_call" | custom-call | tf_op jit(solution)/shard_map/cond/branch_0_fun/while/body/eval_jaxpr/step/pallas_call | solution.py:505
  168.1 27.1 %all_to_all.43 = f32[512,1,128]{2,1,0:T(1,128)S(1)} all-to-all(f32[512,1,128]{2,1,0:T(1,128)} %bitcast.2), channel_id=1, replica_groups=mesh['gx'=8,'gy'=64] {'gx','gy'}, dimensions={0} | all-to-all | bytes 524288 | tf_op jit(solution)/shard_map/cond/branch_0_fun/all_to_all | solution.py:542
  195.2 1.0 finish.1
  196.3 0.0 copy-start.8
  196.3 0.6 copy-done.8
  196.9 0.0 copy-start.9
  196.9 0.6 copy-done.9
  (6 shorter events, 0.1 us)
Async XLA Ops:
  0.6 74.5 %copy-start.4 = (s32[1,2,4]{2,1,0:T(2,128)S(1)}, s32[1,2,4]{2,1,0:T(2,128)}, u32[]{:S(2)}) copy-start(s32[1,2,4]{2,1,0:T(2,128)} %refs_0_.1) | copy-start | bytes 100
  0.6 74.5 %copy-start.5 = (s32[1,2,4]{2,1,0:T(2,128)S(1)}, s32[1,2,4]{2,1,0:T(2,128)}, u32[]{:S(2)}) copy-start(s32[1,2,4]{2,1,0:T(2,128)} %refs_1_.1) | copy-start | bytes 100
  0.7 74.5 %copy-start.6 = (s32[1,2]{1,0:T(1,128)S(1)}, s32[1,2]{1,0:T(1,128)}, u32[]{:S(2)}) copy-start(s32[1,2]{1,0:T(1,128)} %refs_2_.1) | copy-start | bytes 28
  0.7 74.5 %copy-start.7 = (s32[1,2]{1,0:T(1,128)S(1)}, s32[1,2]{1,0:T(1,128)}, u32[]{:S(2)}) copy-start(s32[1,2]{1,0:T(1,128)} %refs_3_.1) | copy-start | bytes 28
  0.7 0.8 copy-start
  1.4 0.7 copy-start.1
  2.1 0.7 copy-start.2
  2.8 0.7 copy-start.3
  30.2 44.9 %all-to-all-start.6 = ((f32[512,2,128]{2,1,0:T(2,128)}), f32[512,2,128]{2,1,0:T(2,128)S(1)}, u32[]{:S(2)}, u32[]{:S(2)}) async-start(f32[512,2,128]{2,1,0:T(2,128)} %bitcast.16), calls=%async_computation.6 | async-start | bytes 1048576 | tf_op jit(solution)/shard_map/all_to_all | solution.py:542
  79.5 25.4 %all-to-all-start.4 = ((f32[512,1,128]{2,1,0:T(1,128)}), f32[512,1,128]{2,1,0:T(1,128)S(1)}, u32[]{:S(2)}, u32[]{:S(2)}) async-start(f32[512,1,128]{2,1,0:T(1,128)} %bitcast.27), calls=%async_computation.4 | async-start | bytes 524288 | tf_op jit(solution)/shard_map/cond/branch_0_fun/while/body/eval_jaxpr/all_to_all | solution.py:542
  108.7 25.9 %all-to-all-start.4 = ((f32[512,1,128]{2,1,0:T(1,128)}), f32[512,1,128]{2,1,0:T(1,128)S(1)}, u32[]{:S(2)}, u32[]{:S(2)}) async-start(f32[512,1,128]{2,1,0:T(1,128)} %bitcast.27), calls=%async_computation.4 | async-start | bytes 524288 | tf_op jit(solution)/shard_map/cond/branch_0_fun/while/body/eval_jaxpr/all_to_all | solution.py:542
  138.4 25.9 %all-to-all-start.4 = ((f32[512,1,128]{2,1,0:T(1,128)}), f32[512,1,128]{2,1,0:T(1,128)S(1)}, u32[]{:S(2)}, u32[]{:S(2)}) async-start(f32[512,1,128]{2,1,0:T(1,128)} %bitcast.27), calls=%async_computation.4 | async-start | bytes 524288 | tf_op jit(solution)/shard_map/cond/branch_0_fun/while/body/eval_jaxpr/all_to_all | solution.py:542
  196.3 0.6 copy-start.8
  196.9 0.6 copy-start.9
where the time goes:
time: 198 us; the launch traced here: 197 us
  waiting for transfers between devices  74.7 us (38%)
  starting transfers between devices  47.4 us (24%)
  Pallas kernels  42.7 us (22%)
  blocking collectives  27.1 us (14%)
  local copies, waits for them, and re-layouts  4.12 us (2%)
    all_to_all x4, waiting for transfers between devices, exchange(): got = lax.all_to_all(sent, axes, split_axis=0, concat_axis=0, tiled=True)  74.7 us
    all_to_all x4, starting transfers between devices, exchange(): got = lax.all_to_all(sent, axes, split_axis=0, concat_axis=0, tiled=True)  47.4 us
    pallas_call x6, Pallas kernels, call(): pl.pallas_call(body, name=name, in_specs=[SMEM] * len(scalars) + (specs o...  42.7 us
    all_to_all x1, blocking collectives, exchange(): got = lax.all_to_all(sent, axes, split_axis=0, concat_axis=0, tiled=True)  27.1 us
    unnamed x20, local copies, waits for them, and re-layouts  4.06 us
  transfers between devices with their start and end apart: 4, of which 4 were waited for; matrix products, arithmetic and copies ran while one was open for 0% of the time, Pallas kernels for 0%

commit v1 on v0

--- a/solution.py
+++ b/solution.py
@@ -22,6 +22,8 @@
 PIVOT = 16
 CELL_PAD = 128
 TRACE_PAD = 152
+VALID_SLAB = ELEM_DEV
+PLACE_SLAB = ELEM_DEV + 1
 LOAD_LANE = TRACE_DOFS
 WIDE = 256
 
@@ -198,21 +200,20 @@
 
 
 def condense_kernel(
-    coeffs_ref,
     owned_ref,
     remote_ref,
     lower_ref,
     upper_ref,
     basis_ref,
-    loads_ref,
-    faces_ref,
-    codes_ref,
-    place_ref,
+    coeffs_in_ref,
+    loads_in_ref,
+    faces_in_ref,
+    codes_in_ref,
+    place_in_ref,
     schur_ref,
     fields_ref,
     pick_ref,
     pick_t_ref,
-    valid_ref,
     bucket_ref,
     shifted_ref,
     panel_ref,
@@ -221,28 +222,58 @@
     diag_ref,
     load_ref,
     terms_ref,
+    coeffs_ref,
+    loads_ref,
+    faces_ref,
+    codes_ref,
+    place_ref,
     copies,
+    small_copies,
 ):
     links = Links(owned_ref, remote_ref, lower_ref, upper_ref)
     width = CELL_PAD + WIDE
 
-    def copy_in(k):
-        return pltpu.make_async_copy(basis_ref.at[k], terms_ref.at[k], copies.at[k])
-
+    small = [
+        pltpu.make_async_copy(source, target, small_copies.at[n])
+        for n, (source, target) in enumerate(
+            (
+                (coeffs_in_ref, coeffs_ref),
+                (loads_in_ref, loads_ref),
+                (faces_in_ref, faces_ref),
+                (codes_in_ref, codes_ref),
+                (place_in_ref, place_ref),
+            )
+        )
+    ]
+
+    def copy_in(k, part):
+        rows = slice(0, 128) if part == 0 else slice(128, LOCAL_DOFS)
+        return pltpu.make_async_copy(basis_ref.at[k, rows], terms_ref.at[k, rows], copies.at[part, k])
+
+    small[0].start()
     for k in range(TERMS):
-        copy_in(k).start()
-
-    def shift(k, carry):
-        copy_in(k).wait()
+        copy_in(k, 0).start()
+    for k in range(TERMS):
+        copy_in(k, 1).start()
+    for copy in small[1:]:
+        copy.start()
+
+    def shift_cells(k, carry):
+        copy_in(k, 0).wait()
         shifted_ref[k, 0:128, 0:125] = terms_ref[k, 0:128, 0:125]
         shifted_ref[k, 0:128, 125:128] = jnp.zeros((128, 3), f32)
         shifted_ref[k, 0:128, 128:278] = terms_ref[k, 0:128, 125:275]
         shifted_ref[k, 0:128, 278:384] = jnp.zeros((128, 106), f32)
+        return carry
+
+    def shift_traces(k, carry):
+        copy_in(k, 1).wait()
         shifted_ref[k, 128:278, 128:278] = terms_ref[k, 125:275, 125:275]
         shifted_ref[k, 128:280, 278:384] = jnp.zeros((152, 106), f32)
         return carry
 
-    lax.fori_loop(0, TERMS, shift, 0)
+    small[0].wait()
+    lax.fori_loop(0, TERMS, shift_cells, 0)
 
     def cell_rows(g, carry):
         at = pl.ds(pl.multiple_of(g * 8, 8), 8)
@@ -255,6 +286,7 @@
         return carry
 
     lax.fori_loop(0, CELL_PAD // 8, cell_rows, 0)
+    lax.fori_loop(0, TERMS, shift_traces, 0)
 
     def trace_rows(g, carry):
         at = pl.ds(pl.multiple_of(g * 8, 8), 8)
@@ -268,6 +300,8 @@
         return carry
 
     lax.fori_loop(0, TRACE_PAD // 8, trace_rows, 0)
+    for copy in small[1:]:
+        copy.wait()
 
     unit = (iota((3, width), 1) == iota((3, width), 0) + CELL_DOFS).astype(f32)
     load_lane = iota((CELL_PAD, 128), 1) == (CELL_PAD + LOAD_LANE) % 128
@@ -373,12 +407,14 @@
     pick_t_ref[...] = jnp.where(iota((SLOTS, ROWS), 0).astype(f32) == slots_row, 1.0, 0.0).astype(bf16)
     lanes = iota((ROWS, WIDE), 1)
     valid = ((lanes // 32).astype(f32) == codes_col) & (lanes % 32 < FACE_DOFS)
-    valid_ref[...] = jnp.where(valid, 1.0, 0.0)
+    schur_ref[VALID_SLAB, 0:ROWS] = jnp.where(valid, 1.0, 0.0)
+    schur_ref[PLACE_SLAB, 0:128] = place_ref[0:128].astype(f32)
+    schur_ref[PLACE_SLAB + 1, 0:128] = place_ref[128:256].astype(f32)
 
     inside = iota((ELEM_DEV, WIDE), 1) < TRACE_DOFS
     for n, ref in enumerate((load_ref, diag_ref)):
         values = jnp.where(inside, ref[...].reshape(ELEM_DEV, WIDE), 0.0)
-        fields_ref[n] = collect(values, pick_t_ref[...], valid_ref[...], place_ref[...])
+        fields_ref[n] = collect(values, pick_t_ref[...], schur_ref[VALID_SLAB, 0:ROWS], place_ref[...])
     send_fields(fields_ref, links, bucket_ref, False)
 
 
@@ -404,8 +440,10 @@
 
 
 def apply_and_send(r, z, q, links, fixed, partial_ref, bucket_ref, image_ref, wide):
-    schur_ref, pick_ref, pick_t_ref, valid_ref, place_ref = fixed
-    x = spread(z, pick_ref[...], valid_ref[...], place_ref[...])
+    schur_ref, pick_ref, pick_t_ref = fixed
+    valid = schur_ref[VALID_SLAB, 0:ROWS]
+    place = jnp.concatenate([schur_ref[PLACE_SLAB + n, 0:128].astype(bf16) for n in range(2)], axis=0)
+    x = spread(z, pick_ref[...], valid, place)
     pad = jnp.zeros((128 - ELEM_DEV, 128), f32)
     head = jnp.concatenate([x[:, 0:128], pad], axis=0).T
     tail = jnp.concatenate([x[:, 128:256], pad], axis=0).T[: TRACE_PAD - 128]
@@ -417,7 +455,7 @@
     own = iota((FACE_DEV, 128), 1) < FACE_DOFS
     rz = total_of(jnp.where(own, r[:FACE_DEV] * z[:FACE_DEV], 0.0))
     zq = total_of(jnp.where(own, z[:FACE_DEV] * q[:FACE_DEV], 0.0))
-    partial_ref[...] = collect(images, pick_t_ref[...], valid_ref[...], place_ref[...])
+    partial_ref[...] = collect(images, pick_t_ref[...], valid, place)
     rows = [[message(partial_ref, links, m)] for m in range(4)]
     lane = iota((1, 128), 1)
     sums = jnp.where(lane == 25, quad, jnp.where(lane == 26, rz, jnp.where(lane == 27, zq, 0.0)))
@@ -426,7 +464,7 @@
 
 def start_kernel(wide, owned_ref, remote_ref, lower_ref, upper_ref, fields_in_ref, arrived_ref, *refs):
     links = Links(owned_ref, remote_ref, lower_ref, upper_ref)
-    fixed, (state_ref, partial_ref, bucket_ref, clash_ref, fields_ref, image_ref) = refs[:5], refs[5:]
+    fixed, (state_ref, partial_ref, bucket_ref, clash_ref, fields_ref, image_ref) = refs[:3], refs[3:]
     clash_ref[0] = jnp.sum(sum_rows(arrived_ref[...])[:, 25:26])
     fields_ref[...] = fields_in_ref[...]
     for n in range(2):
@@ -465,7 +503,7 @@
 
 def step_kernel(wide, owned_ref, remote_ref, lower_ref, upper_ref, partial_in_ref, arrived_ref, state_in_ref, *refs):
     links = Links(owned_ref, remote_ref, lower_ref, upper_ref)
-    fixed, (state_ref, partial_ref, bucket_ref, work_ref, image_ref) = refs[:5], refs[5:]
+    fixed, (state_ref, partial_ref, bucket_ref, work_ref, image_ref) = refs[:3], refs[3:]
     trace, direction, residual, image, rz, energy = advance(
         wide, links, partial_in_ref, arrived_ref, state_in_ref, work_ref
     )
@@ -501,7 +539,11 @@
     return jax.ShapeDtypeStruct(dims, dtype)
 
 
-def call(body, name, scalars, arrays, outs, scratch, specs=None, out_specs=None, grant=12):
+def kept(*dims, dtype=f32):
+    return shape(*dims, dtype=dtype) if INTERPRET else pltpu.VMEM(dims, dtype)
+
+
+def call(body, name, scalars, arrays, outs, scratch, specs=None, out_specs=None, grant=4):
     return pl.pallas_call(
         body,
         name=name,
@@ -542,18 +584,20 @@
         got = lax.all_to_all(sent, axes, split_axis=0, concat_axis=0, tiled=True)
         return got.reshape(bucket.shape)
 
-    schur, fields, pick, pick_t, valid, bucket = call(
+    def raw(array):
+        return pltpu.with_memory_space_constraint(array, pltpu.HBM)
+
+    schur, fields, pick, pick_t, bucket = call(
         condense_kernel,
         "condense",
-        (coeffs,) + links,
-        (pltpu.with_memory_space_constraint(basis_mats, pltpu.HBM), element_loads, elem_faces.T, orient_codes.T, place),
+        links,
+        (raw(basis_mats), raw(coeffs), raw(element_loads), raw(elem_faces.T), raw(orient_codes.T), raw(place)),
         (
-            shape(ELEM_DEV, TRACE_PAD, WIDE),
-            shape(2, SLOTS, 128),
-            shape(ROWS, SLOTS, dtype=bf16),
-            shape(SLOTS, ROWS, dtype=bf16),
-            shape(ROWS, WIDE),
-            shape(2 * devices, 128),
+            kept(ELEM_DEV + 3, TRACE_PAD, WIDE),
+            kept(2, SLOTS, 128),
+            kept(ROWS, SLOTS, dtype=bf16),
+            kept(SLOTS, ROWS, dtype=bf16),
+            shape(2 * devices, 128) if INTERPRET else pltpu.HBM((2 * devices, 128), f32),
         ),
         (
             (TERMS, CELL_PAD + TRACE_PAD, width),
@@ -563,12 +607,18 @@
             (ELEM_DEV, 1, WIDE),
             (ELEM_DEV, 1, WIDE),
             (TERMS, LOCAL_DOFS, LOCAL_DOFS),
-            pltpu.SemaphoreType.DMA((TERMS,)),
+            pltpu.SMEM((ELEM_DEV, TERMS), f32),
+            (ELEM_DEV, LOCAL_DOFS),
+            pltpu.VMEM((6, ELEM_DEV), jnp.int32),
+            pltpu.VMEM((6, ELEM_DEV), jnp.int32),
+            pltpu.VMEM((WIDE, WIDE), bf16),
+            pltpu.SemaphoreType.DMA((2, TERMS)),
+            pltpu.SemaphoreType.DMA((5,)),
         ),
-        specs=[HBM] + [VMEM] * 4,
-        grant=44,
+        specs=[HBM] * 6,
+        grant=28,
     )
-    fixed = (schur, pick, pick_t, valid, place)
+    fixed = (schur, pick, pick_t)
 
     def start(arrived, wide):
         return call(
@@ -576,7 +626,7 @@
             "start_wide" if wide else "start",
             links,
             (fields, arrived) + fixed,
-            (shape(6, SLOTS, 128), shape(SLOTS, 128), shape((1 + wide) * devices, 128), shape(1)),
+            (kept(6, SLOTS, 128), kept(SLOTS, 128), shape((1 + wide) * devices, 128), shape(1)),
             ((2, SLOTS, 128), (ELEM_DEV, WIDE)),
             out_specs=[VMEM] * 3 + [SMEM],
         )
@@ -587,7 +637,7 @@
             "step_wide" if wide else "step",
             links,
             (partial_value, arrived, state) + fixed,
-            (shape(6, SLOTS, 128), shape(SLOTS, 128), shape((1 + wide) * devices, 128)),
+            (kept(6, SLOTS, 128), kept(SLOTS, 128), shape((1 + wide) * devices, 128)),
             ((SLOTS, 128), (ELEM_DEV, WIDE)),
         )
 

time: 198 us -> 195 us (0.985)
  local copies, waits for them, and re-layouts: 4.12 us -> 1.29 us
  starting transfers between devices: 47.4 us -> 49.7 us
  waiting for transfers between devices: 74.7 us -> 72.7 us
    unnamed x20 -> x12, local copies, waits for them, and re-layouts: 4.06 us -> 1.23 us
    all_to_all x4, starting transfers between devices: 47.4 us -> 49.7 us  [exchange(): got = lax.all_to_all(sent, axes, split_axis=0, concat_axis=0, tiled=True)]
where the time goes in v1:
time: 195 us
  waiting for transfers between devices  72.7 us (37%)
  starting transfers between devices  49.7 us (25%)
  Pallas kernels  42.4 us (22%)
  blocking collectives  27.2 us (14%)
    all_to_all x4, waiting for transfers between devices, exchange(): got = lax.all_to_all(sent, axes, split_axis=0, concat_axis=0, tiled=True)  72.7 us
    all_to_all x4, starting transfers between devices, exchange(): got = lax.all_to_all(sent, axes, split_axis=0, concat_axis=0, tiled=True)  49.7 us
    pallas_call x6, Pallas kernels, call(): pl.pallas_call(body, name=name, in_specs=[SMEM] * len(scalars) + (specs o...  42.4 us
    all_to_all x1, blocking collectives, exchange(): got = lax.all_to_all(sent, axes, split_axis=0, concat_axis=0, tiled=True)  27.2 us
  transfers between devices with their start and end apart: 4, of which 4 were waited for; matrix products, arithmetic and copies ran while one was open for 0% of the time, Pallas kernels for 0%

profile of v1, /device:TPU:1, one launch (start us, length us, event | category | flops | bytes accessed | tf_op | source)
XLA Modules:
  0.0 194.8 jit_solution(7383664904452945067)
XLA Ops:
  0.6 0.0 copy-start
  0.6 0.0 copy-start.1
  0.7 0.0 copy-start.2
  0.7 0.0 copy-start.3
  0.7 27.5 %condense.1 = (f32[19,152,256]{2,1,0:T(8,128)S(1)}, f32[2,72,128]{2,1,0:T(8,128)S(1)}, bf16[96,72]{1,0:T(8,128)(2,1)S(1)}, bf16[72,96]{1,0:T(8,128)(2,1)S(1)}, f32[1024,128]{1,0:T(8,128)}) custom-call(s32[1,2,4]{2,1,0:T(2,128)} %refs_0_.1, s32[1,2,4]{2,1,0:T(2,128)} %refs_1_.1, s32[1,2]{1,0:T(1,128)} %refs_2_.1, s32[1,2]{1,0:T(1,128)} %refs_3_.1, ...), custom_call_target="tpu_custom_call" | custom-call | tf_op jit(solution)/shard_map/condense/pallas_call | solution.py:547
  28.2 24.2 %all-to-all-start.6 = ((f32[512,2,128]{2,1,0:T(2,128)}), f32[512,2,128]{2,1,0:T(2,128)}, u32[]{:S(2)}, u32[]{:S(2)}) async-start(f32[512,2,128]{2,1,0:T(2,128)} %bitcast.37), calls=%async_computation.6 | async-start | bytes 1048576 | tf_op jit(solution)/shard_map/all_to_all | solution.py:584
  52.4 20.7 %all-to-all-done.6 = f32[512,2,128]{2,1,0:T(2,128)} async-done(((f32[512,2,128]{2,1,0:T(2,128)}), f32[512,2,128]{2,1,0:T(2,128)}, u32[]{:S(2)}, u32[]{:S(2)}) %all-to-all-start.6) | async-done | bytes 524320 | tf_op jit(solution)/shard_map/all_to_all | solution.py:584
  73.2 0.0 copy-done
  73.2 0.0 copy-done.1
  73.2 0.0 copy-done.2
  73.2 0.0 copy-done.3
  73.2 3.8 %start.1 = (f32[6,72,128]{2,1,0:T(8,128)S(1)}, f32[72,128]{1,0:T(8,128)S(1)}, f32[512,128]{1,0:T(8,128)}, f32[1]{0:T(128)}) custom-call(s32[1,2,4]{2,1,0:T(2,128)S(1)} %copy-done, s32[1,2,4]{2,1,0:T(2,128)S(1)} %copy-done.1, s32[1,2]{1,0:T(1,128)S(1)} %copy-done.2, s32[1,2]{1,0:T(1,128)S(1)} %copy-done.3, f32[2,72,128]{2,1,0:T(8,128)S(1)} %get-tuple-element.190.refs_4_, ...), custom_call_target="tpu_custom_call" | custom-call | tf_op jit(solution)/shard_map/start/pallas_call | solution.py:547
  77.6 116.0 %conditional.1 = ((f32[25,64]{1,0:T(8,128)S(1)}, f32[25,64]{1,0:T(8,128)S(1)})) conditional(s32[]{:T(128)} %bitcast.18, (s32[1,2,4]{2,1,0:T(2,128)S(1)}, s32[1,2,4]{2,1,0:T(2,128)S(1)}, s32[1,2]{1,0:T(1,128)S(1)}, s32[1,2]{1,0:T(1,128)S(1)}, f32[19,152,256]{2,1,0:T(8,128)S(1)}, /*index=5*/bf16[96,72]{1,0:T(8,128)(2,1)S(1)}, ...), branch_computations={%region_0.0_spmd, %region_3.0_spmd} | conditional | flops 2 | bytes 14723381 | solution.py:677
  77.6 87.7 %while.26 = (s32[]{:T(128)}, f32[6,72,128]{2,1,0:T(8,128)S(1)}, f32[72,128]{1,0:T(8,128)S(1)}, f32[512,128]{1,0:T(8,128)}, s32[1,2,4]{2,1,0:T(2,128)S(1)}, /*ind...) while((s32[]{:T(128)}, f32[6,72,128]{2,1,0:T(8,128)S(1)}, ...), condition=%wide.region_2.0_spmd, body=%wide.region_1.0_spmd.sunk | while | flops 2 | bytes 1302677 | solution.py:661
  77.6 8.3 %all-to-all-start.4 = ((f32[512,1,128]{2,1,0:T(1,128)}), f32[512,1,128]{2,1,0:T(1,128)S(1)}, u32[]{:S(2)}, u32[]{:S(2)}) async-start(f32[512,1,128]{2,1,0:T(1,128)} %bitcast.35), calls=%async_computation.4 | async-start | bytes 524288 | tf_op jit(solution)/shard_map/cond/branch_0_fun/while/body/eval_jaxpr/all_to_all | solution.py:584
  85.9 17.0 %all-to-all-done.4 = f32[512,1,128]{2,1,0:T(1,128)S(1)} async-done(((f32[512,1,128]{2,1,0:T(1,128)}), f32[512,1,128]{2,1,0:T(1,128)S(1)}, u32[]{:S(2)}, u32[]{:S(2)}) %all-to-all-start.4) | async-done | bytes 262176 | tf_op jit(solution)/shard_map/cond/branch_0_fun/while/body/eval_jaxpr/all_to_all | solution.py:584
  103.0 3.4 %step.1 = (f32[6,72,128]{2,1,0:T(8,128)S(1)}, f32[72,128]{1,0:T(8,128)S(1)}, f32[512,128]{1,0:T(8,128)}) custom-call(s32[1,2,4]{2,1,0:T(2,128)S(1)} %get-tuple-element.477.refs_0_, s32[1,2,4]{2,1,0:T(2,128)S(1)} %get-tuple-element.478.refs_1_, s32[1,2]{1,0:T(1,128)S(1)} %get-tuple-element.479.refs_2_, s32[1,2]{1,0:T(1,128)S(1)} %get-tuple-element.480.refs_3_, ...), custom_call_target="tpu_custom_call" | custom-call | tf_op jit(solution)/shard_map/cond/branch_0_fun/while/body/eval_jaxpr/step/pallas_call | solution.py:547
  106.4 8.6 %all-to-all-start.4 = ((f32[512,1,128]{2,1,0:T(1,128)}), f32[512,1,128]{2,1,0:T(1,128)S(1)}, u32[]{:S(2)}, u32[]{:S(2)}) async-start(f32[512,1,128]{2,1,0:T(1,128)} %bitcast.35), calls=%async_computation.4 | async-start | bytes 524288 | tf_op jit(solution)/shard_map/cond/branch_0_fun/while/body/eval_jaxpr/all_to_all | solution.py:584
  115.0 17.5 %all-to-all-done.4 = f32[512,1,128]{2,1,0:T(1,128)S(1)} async-done(((f32[512,1,128]{2,1,0:T(1,128)}), f32[512,1,128]{2,1,0:T(1,128)S(1)}, u32[]{:S(2)}, u32[]{:S(2)}) %all-to-all-start.4) | async-done | bytes 262176 | tf_op jit(solution)/shard_map/cond/branch_0_fun/while/body/eval_jaxpr/all_to_all | solution.py:584
  132.5 3.4 %step.1 = (f32[6,72,128]{2,1,0:T(8,128)S(1)}, f32[72,128]{1,0:T(8,128)S(1)}, f32[512,128]{1,0:T(8,128)}) custom-call(s32[1,2,4]{2,1,0:T(2,128)S(1)} %get-tuple-element.477.refs_0_, s32[1,2,4]{2,1,0:T(2,128)S(1)} %get-tuple-element.478.refs_1_, s32[1,2]{1,0:T(1,128)S(1)} %get-tuple-element.479.refs_2_, s32[1,2]{1,0:T(1,128)S(1)} %get-tuple-element.480.refs_3_, ...), custom_call_target="tpu_custom_call" | custom-call | tf_op jit(solution)/shard_map/cond/branch_0_fun/while/body/eval_jaxpr/step/pallas_call | solution.py:547
  135.9 8.6 %all-to-all-start.4 = ((f32[512,1,128]{2,1,0:T(1,128)}), f32[512,1,128]{2,1,0:T(1,128)S(1)}, u32[]{:S(2)}, u32[]{:S(2)}) async-start(f32[512,1,128]{2,1,0:T(1,128)} %bitcast.35), calls=%async_computation.4 | async-start | bytes 524288 | tf_op jit(solution)/shard_map/cond/branch_0_fun/while/body/eval_jaxpr/all_to_all | solution.py:584
  144.4 17.5 %all-to-all-done.4 = f32[512,1,128]{2,1,0:T(1,128)S(1)} async-done(((f32[512,1,128]{2,1,0:T(1,128)}), f32[512,1,128]{2,1,0:T(1,128)S(1)}, u32[]{:S(2)}, u32[]{:S(2)}) %all-to-all-start.4) | async-done | bytes 262176 | tf_op jit(solution)/shard_map/cond/branch_0_fun/while/body/eval_jaxpr/all_to_all | solution.py:584
  161.9 3.4 %step.1 = (f32[6,72,128]{2,1,0:T(8,128)S(1)}, f32[72,128]{1,0:T(8,128)S(1)}, f32[512,128]{1,0:T(8,128)}) custom-call(s32[1,2,4]{2,1,0:T(2,128)S(1)} %get-tuple-element.477.refs_0_, s32[1,2,4]{2,1,0:T(2,128)S(1)} %get-tuple-element.478.refs_1_, s32[1,2]{1,0:T(1,128)S(1)} %get-tuple-element.479.refs_2_, s32[1,2]{1,0:T(1,128)S(1)} %get-tuple-element.480.refs_3_, ...), custom_call_target="tpu_custom_call" | custom-call | tf_op jit(solution)/shard_map/cond/branch_0_fun/while/body/eval_jaxpr/step/pallas_call | solution.py:547
  165.3 27.2 %all_to_all.43 = f32[512,1,128]{2,1,0:T(1,128)S(1)} all-to-all(f32[512,1,128]{2,1,0:T(1,128)} %bitcast.36), channel_id=1, replica_groups=mesh['gx'=8,'gy'=64] {'gx','gy'}, dimensions={0} | all-to-all | bytes 524288 | tf_op jit(solution)/shard_map/cond/branch_0_fun/all_to_all | solution.py:584
  192.5 1.0 finish.1
  193.6 0.0 copy-start.4
  193.6 0.6 copy-done.4
  194.2 0.0 copy-start.5
  194.2 0.6 copy-done.5
  (6 shorter events, 0.1 us)
Async XLA Ops:
  0.6 72.5 %copy-start = (s32[1,2,4]{2,1,0:T(2,128)S(1)}, s32[1,2,4]{2,1,0:T(2,128)}, u32[]{:S(2)}) copy-start(s32[1,2,4]{2,1,0:T(2,128)} %refs_0_.1) | copy-start | bytes 100
  0.6 72.5 %copy-start.1 = (s32[1,2,4]{2,1,0:T(2,128)S(1)}, s32[1,2,4]{2,1,0:T(2,128)}, u32[]{:S(2)}) copy-start(s32[1,2,4]{2,1,0:T(2,128)} %refs_1_.1) | copy-start | bytes 100
  0.7 72.5 %copy-start.2 = (s32[1,2]{1,0:T(1,128)S(1)}, s32[1,2]{1,0:T(1,128)}, u32[]{:S(2)}) copy-start(s32[1,2]{1,0:T(1,128)} %refs_2_.1) | copy-start | bytes 28
  0.7 72.5 %copy-start.3 = (s32[1,2]{1,0:T(1,128)S(1)}, s32[1,2]{1,0:T(1,128)}, u32[]{:S(2)}) copy-start(s32[1,2]{1,0:T(1,128)} %refs_3_.1) | copy-start | bytes 28
  28.2 45.0 %all-to-all-start.6 = ((f32[512,2,128]{2,1,0:T(2,128)}), f32[512,2,128]{2,1,0:T(2,128)}, u32[]{:S(2)}, u32[]{:S(2)}) async-start(f32[512,2,128]{2,1,0:T(2,128)} %bitcast.37), calls=%async_computation.6 | async-start | bytes 1048576 | tf_op jit(solution)/shard_map/all_to_all | solution.py:584
  77.6 25.4 %all-to-all-start.4 = ((f32[512,1,128]{2,1,0:T(1,128)}), f32[512,1,128]{2,1,0:T(1,128)S(1)}, u32[]{:S(2)}, u32[]{:S(2)}) async-start(f32[512,1,128]{2,1,0:T(1,128)} %bitcast.35), calls=%async_computation.4 | async-start | bytes 524288 | tf_op jit(solution)/shard_map/cond/branch_0_fun/while/body/eval_jaxpr/all_to_all | solution.py:584
  106.4 26.0 %all-to-all-start.4 = ((f32[512,1,128]{2,1,0:T(1,128)}), f32[512,1,128]{2,1,0:T(1,128)S(1)}, u32[]{:S(2)}, u32[]{:S(2)}) async-start(f32[512,1,128]{2,1,0:T(1,128)} %bitcast.35), calls=%async_computation.4 | async-start | bytes 524288 | tf_op jit(solution)/shard_map/cond/branch_0_fun/while/body/eval_jaxpr/all_to_all | solution.py:584
  135.9 26.0 %all-to-all-start.4 = ((f32[512,1,128]{2,1,0:T(1,128)}), f32[512,1,128]{2,1,0:T(1,128)S(1)}, u32[]{:S(2)}, u32[]{:S(2)}) async-start(f32[512,1,128]{2,1,0:T(1,128)} %bitcast.35), calls=%async_computation.4 | async-start | bytes 524288 | tf_op jit(solution)/shard_map/cond/branch_0_fun/while/body/eval_jaxpr/all_to_all | solution.py:584
  193.6 0.6 copy-start.4
  194.2 0.6 copy-start.5
